TPU v7x, 32 devices: a whole 2x2x4 slice. The times are simulated.
32 devices in a mesh: groups: 2 (over y), tensor: 4 (over z), frames: 4 (over x, core).
Axes of the slice: x: 2, y: 2, z: 4, core: 2. Of those that a mesh axis runs over, the one named last changes fastest.
Arguments:
- patches: bfloat16 [256, 16, 3072], P('tensor', ('groups', 'frames')), parts along dimension 1, may hold values from -12 to 12
- ln_gain: float32 [3072], replicated, may hold values from 0.5 to 1.5
- in_weight: bfloat16 [3072, 4, 768], P('frames', 'tensor'), may hold values from -0.109375 to 0.109375
- q_gain: float32 [4, 128], P('tensor'), may hold values from 0.1 to 1.9
- k_gain: float32 [4, 128], P('tensor'), may hold values from 0.1 to 1.9
- out_weight: bfloat16 [4, 512, 3072], P('tensor', None, 'frames'), may hold values from -0.25 to 0.25
Outputs:
- encoded: bfloat16 [256, 16, 3072], P('tensor', ('groups', 'frames')), parts along dimension 1
There are 2 independent parts, one for each index of `groups`. A program takes and returns all parts, laid end to end along the dimension named above; an argument that names none is the same for every part. Nothing has to cross between parts.
All inputs are finite; a program needn't handle non-finite values.
Results may differ from a plain program's by a relative error of at most 0.022.
Values may be sent and summed in bfloat16 or wider, within the bound.
No kernel may reach another device: no remote copies, remote signals or barrier semaphores. Data moves between devices by JAX's collectives and lax.ppermute only.
A program may use at most 64 MiB of HBM per device.

v0:
```python
import math
import jax
import jax.numpy as jnp
from jax import lax
from jax.sharding import PartitionSpec as P


def layer_norm(values, gain_vec):
    mean_val = jnp.mean(values, axis=-1, keepdims=True)
    centered = values - mean_val
    variance = jnp.mean(centered * centered, axis=-1, keepdims=True)
    return centered * lax.rsqrt(variance + 1e-06) * gain_vec


def local(patches, ln_gain, in_weight, q_gain, k_gain, out_weight):
    head_dim = q_gain.shape[1]
    normed = layer_norm(patches.astype(jnp.float32), ln_gain).astype(jnp.bfloat16)
    in_local = in_weight[:, 0, :]
    out_local = out_weight[0]
    every_patch = lax.all_gather(normed, "tensor", axis=0, tiled=True)
    joined_cols = jnp.einsum(
        "qye,ea->qya",
        every_patch,
        lax.all_gather(in_local, "frames", axis=0, tiled=True),
        preferred_element_type=jnp.float32,
    )
    query_slice = layer_norm(joined_cols[..., :head_dim], q_gain[0])
    key_slice = layer_norm(joined_cols[..., head_dim : 2 * head_dim], k_gain[0])
    value_slice = joined_cols[..., 2 * head_dim : 3 * head_dim]
    hidden = jax.nn.gelu(joined_cols[..., 3 * head_dim :], approximate=False)
    prepared = jnp.concatenate([query_slice, key_slice, value_slice, hidden], axis=-1).astype(
        jnp.bfloat16
    )
    query_slice = prepared[..., :head_dim]
    key_slice = prepared[..., head_dim : 2 * head_dim]
    value_slice = prepared[..., 2 * head_dim : 3 * head_dim]
    attention_logits = jnp.einsum(
        "ldg,bdg->dlb", query_slice, key_slice, preferred_element_type=jnp.float32
    ) * (1.0 / math.sqrt(head_dim))
    exponent_scores = jnp.exp(attention_logits)
    softmax_total = jnp.sum(exponent_scores, axis=-1)
    attention_output = jnp.einsum(
        "jdl,ljg->djg",
        exponent_scores.astype(jnp.bfloat16),
        value_slice,
        preferred_element_type=jnp.float32,
    )
    attention_output = attention_output / jnp.transpose(softmax_total)[:, :, None]
    blended_rows = jnp.concatenate(
        [attention_output.astype(jnp.bfloat16), prepared[..., 3 * head_dim :]], axis=-1
    )
    combined_output = lax.all_gather(out_local, "frames", axis=1, tiled=True)
    summed = lax.psum_scatter(
        jnp.einsum(
            "vto,ox->vtx", blended_rows, combined_output, preferred_element_type=jnp.float32
        ).astype(jnp.bfloat16),
        "tensor",
        scatter_dimension=0,
        tiled=True,
    ).astype(jnp.float32)
    return (patches.astype(jnp.float32) + summed).astype(jnp.bfloat16)


def solution(mesh):
    return jax.shard_map(
        local,
        mesh=mesh,
        in_specs=(
            P("tensor", ("groups", "frames"), None),
            P(),
            P("frames", "tensor", None),
            P("tensor", None),
            P("tensor", None),
            P("tensor", None, "frames"),
        ),
        out_specs=P("tensor", ("groups", "frames"), None),
        check_vma=False,
    )
```

profile of v0, /device:TPU:0, one launch (start us, length us, event | category | flops | bytes accessed | tf_op | source)
XLA Modules:
  0.0 220.3 jit_solution(9089769881547310153)
XLA Ops:
  6.5 0.0 copy-start
  6.5 0.0 copy-start.1
  6.5 0.0 all-gather.6.cloned.1.call-start
  6.5 1.4 convert_reduce_fusion
  7.9 1.5 fusion.5
  9.5 0.0 copy-done
  9.5 0.0 copy-done.1
  9.5 1.2 fusion.7
  10.7 0.0 all-gather.6.cloned.1.call-update
  10.7 0.0 all-gather.8.cloned.1.call-start
  10.8 0.7 all-gather.8.cloned.1.call-update
  11.5 0.0 all-gather.10.cloned.1.call-start
  11.5 0.7 all-gather.10.cloned.1.call-update
  12.2 0.0 copy-start.2
  12.2 0.0 copy-start.3
  12.2 0.0 reduce-scatter.2.cloned.1.call-start
  12.3 64.8 %all-gather.6.cloned.1.call-done = bf16[256,2,3072]{2,0,1:T(8,128)(2,1)} async-done(((bf16[64,2,3072]{2,0,1:T(8,128)(2,1)}), bf16[256,2,3072]{2,0,1:T(8,128)(2,1)}) %all-gather.6.cloned.1.call-update) | async-done | bytes 3145744 | tf_op jit(solution)/shard_map/all_gather | solution.py:20
  77.0 37.7 %all-gather.8.cloned.1.call-done = bf16[3072,1,768]{2,0,1:T(8,128)(2,1)} async-done(((bf16[768,1,768]{2,0,1:T(8,128)(2,1)}), bf16[3072,1,768]{2,0,1:T(8,128)(2,1)}) %all-gather.8.cloned.1.call-update) | async-done | bytes 4718608 | tf_op jit(solution)/shard_map/all_gather | solution.py:24
  114.7 5.9 %fusion = f32[256,2,768]{2,0,1:T(8,128)S(1)} fusion(bf16[256,2,3072]{2,0,1:T(8,128)(2,1)} %all-gather.6.cloned.1.call-done, bf16[3072,1,768]{2,0,1:T(8,128)(2,1)} %all-gather.8.cloned.1.call-done), kind=kOutput, calls=%fused_computation | convolution fusion | flops 2415919104 | bytes 9437184 | tf_op jit(solution)/shard_map/qye,ea->qya/dot_general | solution.py:21
  120.6 0.2 slice_reduce_fusion.1
  120.8 0.4 multiply_reduce_fusion.1
  121.2 0.0 copy-done.2
  121.3 0.0 copy-done.3
  121.3 0.5 fusion.33
  121.8 0.3 fusion.11
  122.0 1.7 fusion.14
  123.8 21.1 %all-gather.10.cloned.1.call-done = bf16[1,512,3072]{2,1,0:T(8,128)(2,1)} async-done(((bf16[1,512,768]{2,1,0:T(8,128)(2,1)}), bf16[1,512,3072]{2,1,0:T(8,128)(2,1)}) %all-gather.10.cloned.1.call-update) | async-done | bytes 3145744 | tf_op jit(solution)/shard_map/all_gather | solution.py:52
  144.8 5.4 %convolution_convert_fusion = bf16[256,2,3072]{2,0,1:T(8,128)(2,1)} fusion(bf16[1,512,3072]{2,1,0:T(8,128)(2,1)} %all-gather.10.cloned.1.call-done, bf16[256,2,384]{2,0,1:T(8,128)(2,1)S(1)} %fusion.14, bf16[256,2,128]{2,0,1:T(8,128)(2,1)S(1)} %fusion.11), kind=kOutput, calls=%fused_computation.2 | convolution fusion | flops 1613234176 | bytes 6815744 | tf_op jit(solution)/shard_map/vto,ox->vtx/dot_general | solution.py:54
  150.2 0.0 reduce-scatter.2.cloned.1.call-update
  150.2 60.6 %reduce-scatter.2.cloned.1.call-done = bf16[64,2,3072]{2,0,1:T(8,128)(2,1)} async-done(((bf16[256,2,3072]{2,0,1:T(8,128)(2,1)}), bf16[64,2,3072]{2,0,1:T(8,128)(2,1)}) %reduce-scatter.2.cloned.1.call-update) | async-done | bytes 786448 | tf_op jit(solution)/shard_map/reduce_scatter | solution.py:53
  210.8 1.3 fusion.8
  212.1 1.7 copy.8
  (5 shorter events, 0.0 us)
Async XLA Ops:
  6.5 2.9 %copy-start = (bf16[64,2,3072]{2,1,0:T(2,128)(2,1)S(1)}, bf16[64,2,3072]{2,1,0:T(2,128)(2,1)}, u32[]{:S(2)}) copy-start(bf16[64,2,3072]{2,1,0:T(2,128)(2,1)} %param.6) | copy-start | bytes 2359300
  6.5 2.9 %copy-start.1 = (f32[3072]{0:T(1024)S(1)}, f32[3072]{0:T(1024)}, u32[]{:S(2)}) copy-start(f32[3072]{0:T(1024)} %param.7) | copy-start | bytes 36868
  6.5 70.5 %all-gather.6.cloned.1.call-start = ((), (), s32[]{:S(2)}) async-start(), calls=%async_computation.1 | async-start | bytes 3932160 | tf_op jit(solution)/shard_map/all_gather | solution.py:20
  10.7 104.0 %all-gather.8.cloned.1.call-start = ((), (), s32[]{:S(2)}) async-start(), calls=%async_computation.3 | async-start | bytes 5898240 | tf_op jit(solution)/shard_map/all_gather | solution.py:24
  11.5 133.3 %all-gather.10.cloned.1.call-start = ((), (), s32[]{:S(2)}) async-start(), calls=%async_computation.4 | async-start | bytes 3932160 | tf_op jit(solution)/shard_map/all_gather | solution.py:52
  12.2 109.0 %copy-start.2 = (f32[1,128]{1,0:T(1,128)S(1)}, f32[1,128]{1,0:T(1,128)}, u32[]{:S(2)}) copy-start(f32[1,128]{1,0:T(1,128)} %param.10) | copy-start | bytes 1540
  12.2 109.0 %copy-start.3 = (f32[1,128]{1,0:T(1,128)S(1)}, f32[1,128]{1,0:T(1,128)}, u32[]{:S(2)}) copy-start(f32[1,128]{1,0:T(1,128)} %param.9) | copy-start | bytes 1540
  12.2 198.5 %reduce-scatter.2.cloned.1.call-start = ((), (), s32[]{:S(2)}) async-start(), calls=%async_computation.2 | async-start | bytes 3932160 | tf_op jit(solution)/shard_map/reduce_scatter | solution.py:53
Sparse Core Ops, SparseCore 0:
  10.8 66.1 all-gather.5
  78.6 36.0 all-gather.7
  116.3 28.5 all-gather.9
  150.3 60.3 reduce-scatter.1
where the time goes:
time: 221 us; the launch traced here: 220 us
  waiting for transfers between devices  185 us (84%)
  between operations  13.2 us (6%)
  matrix products  12 us (5%)
  other arithmetic  7.81 us (4%)
    all_gather x1, waiting for transfers between devices, local(): every_patch = lax.all_gather(normed, 'tensor', axis=0, tiled=True)  64.8 us
    reduce_scatter x1, waiting for transfers between devices, local(): lax.psum_scatter(jnp.einsum('vto,ox->vtx', blended_rows, combined_output,...  60.6 us
    all_gather x1, waiting for transfers between devices, local(): lax.all_gather(in_local, 'frames', axis=0, tiled=True)  37.7 us
    all_gather x1, waiting for transfers between devices, local(): combined_output = lax.all_gather(out_local, 'frames', axis=1, tiled=True)  21.1 us
    dot_general x1, matrix products, local(): jnp.einsum('qye,ea->qya', every_patch, lax.all_gather(in_local, 'frames',...  5.89 us
    dot_general x1, matrix products, local(): jnp.einsum('vto,ox->vtx', blended_rows, combined_output, preferred_elemen...  5.36 us
  transfers between devices with their start and end apart: 4, of which 4 were waited for; matrix products, arithmetic and copies ran while one was open for 4% of the time, Pallas kernels for 0%

commit v1 on v0

--- a/solution.py
+++ b/solution.py
@@ -49,7 +49,14 @@
     blended_rows = jnp.concatenate(
         [attention_output.astype(jnp.bfloat16), prepared[..., 3 * head_dim :]], axis=-1
     )
-    combined_output = lax.all_gather(out_local, "frames", axis=1, tiled=True)
+    ring = [out_local]
+    for hop in range(3):
+        ring.append(lax.ppermute(ring[-1], "frames", [(dev, (dev + 1) % 4) for dev in range(4)]))
+    combined_output = jnp.roll(
+        jnp.concatenate(ring[::-1], axis=1),
+        (lax.axis_index("frames") + 1) * ring[0].shape[1],
+        axis=1,
+    )
     summed = lax.psum_scatter(
         jnp.einsum(
             "vto,ox->vtx", blended_rows, combined_output, preferred_element_type=jnp.float32

time: 221 us -> 201 us (0.910)
  waiting for transfers between devices: 185 us -> 156 us
  local copies, waits for them, and re-layouts: 1.71 us -> 9.62 us
    all_gather x1, waiting for transfers between devices: 64.8 us -> 22.6 us  [local(): every_patch = lax.all_gather(normed, 'tensor', axis=0, tiled=True)]
    ppermute x0 -> x3, waiting for transfers between devices: none -> 34.4 us  [local(): lax.ppermute(ring[-1], 'frames', [(dev, (dev + 1) % 4) for dev in range(4)])]
    all_gather x1 -> x0, waiting for transfers between devices: 21.1 us -> none  [local(): combined_output = lax.all_gather(out_local, 'frames', axis=1, tiled=True)]
    unnamed x8 -> x15, local copies, waits for them, and re-layouts: 0.02 us -> 6.94 us
  transfers between devices with their start and end apart: 4 -> 6, of which waited for: 4 -> 6; matrix products, arithmetic and copies ran while one was open for 4% -> 4% of each run, Pallas kernels for 0% -> 0%
where the time goes in v1:
time: 201 us
  waiting for transfers between devices  156 us (78%)
  between operations  13.2 us (7%)
  matrix products  12.2 us (6%)
  local copies, waits for them, and re-layouts  9.62 us (5%)
  other arithmetic  8.96 us (4%)
    reduce_scatter x1, waiting for transfers between devices, local(): lax.psum_scatter(jnp.einsum('vto,ox->vtx', blended_rows, combined_output,...  60.6 us
    all_gather x1, waiting for transfers between devices, local(): lax.all_gather(in_local, 'frames', axis=0, tiled=True)  37.7 us
    ppermute x3, waiting for transfers between devices, local(): lax.ppermute(ring[-1], 'frames', [(dev, (dev + 1) % 4) for dev in range(4)])  34.4 us
    all_gather x1, waiting for transfers between devices, local(): every_patch = lax.all_gather(normed, 'tensor', axis=0, tiled=True)  22.6 us
    unnamed x15, local copies, waits for them, and re-layouts  6.94 us
    dot_general x1, matrix products, local(): jnp.einsum('qye,ea->qya', every_patch, lax.all_gather(in_local, 'frames',...  5.89 us
    dot_general x1, matrix products, local(): jnp.einsum('vto,ox->vtx', blended_rows, combined_output, preferred_elemen...  5.55 us
  transfers between devices with their start and end apart: 6, of which 6 were waited for; matrix products, arithmetic and copies ran while one was open for 4% of the time, Pallas kernels for 0%

profile of v1, /device:TPU:0, one launch (start us, length us, event | category | flops | bytes accessed | tf_op | source)
XLA Modules:
  0.0 200.6 jit_solution(6290788865916196688)
XLA Ops:
  6.5 0.0 copy-start.1
  6.5 0.0 all-gather.4.cloned.1.call-start
  6.5 1.4 convert_reduce_fusion
  7.9 1.5 fusion.6
  9.5 2.4 %fusion.8 = bf16[64,2,3072]{2,0,1:T(8,128)(2,1)} fusion(f32[3072]{0:T(1024)} %param.7, f32[64,2]{0,1:T(2,128)S(1)} %add_rsqrt_fusion.2, f32[64,2]{0,1:T(2,128)S(1)} %broadcast_multiply_fusion.2, bf16[64,2,3072]{2,1,0:T(2,128)(2,1)} %param.6), kind=kLoop, calls=%fused_computation.12 | loop fusion | flops 1966080 | bytes 1586176 | tf_op jit(solution)/shard_map/convert_element_type | solution.py:17
  11.8 0.0 all-gather.4.cloned.1.call-update
  11.9 0.0 all-gather.6.cloned.1.call-start
  11.9 0.7 all-gather.6.cloned.1.call-update
  12.6 0.0 reduce-scatter.2.cloned.1.call-start
  12.7 0.0 copy-done.1
  12.7 0.5 collective-permute-start
  13.2 11.6 %collective-permute-done = bf16[512,768]{1,0:T(8,128)(2,1)S(1)} collective-permute-done((bf16[512,768]{1,0:T(8,128)(2,1)S(1)}, bf16[512,768]{1,0:T(8,128)(2,1)S(1)}, u32[]{:S(2)}, u32[]{:S(2)}) %collective-permute-start) | collective-permute-done | bytes 786464 | tf_op jit(solution)/shard_map/ppermute | solution.py:54
  24.8 0.0 collective-permute-start.1
  24.8 11.4 %collective-permute-done.1 = bf16[512,768]{1,0:T(8,128)(2,1)S(1)} collective-permute-done((bf16[512,768]{1,0:T(8,128)(2,1)S(1)}, bf16[512,768]{1,0:T(8,128)(2,1)S(1)}, u32[]{:S(2)}, u32[]{:S(2)}) %collective-permute-start.1) | collective-permute-done | bytes 786464 | tf_op jit(solution)/shard_map/ppermute | solution.py:54
  36.2 0.0 collective-permute-start.2
  36.2 11.4 %collective-permute-done.2 = bf16[512,768]{1,0:T(8,128)(2,1)S(1)} collective-permute-done((bf16[512,768]{1,0:T(8,128)(2,1)S(1)}, bf16[512,768]{1,0:T(8,128)(2,1)S(1)}, u32[]{:S(2)}, u32[]{:S(2)}) %collective-permute-start.2) | collective-permute-done | bytes 786464 | tf_op jit(solution)/shard_map/ppermute | solution.py:54
  47.6 1.0 constant_dynamic-update-slice_fusion.7
  48.6 1.0 constant_dynamic-update-slice_fusion.6
  49.6 1.0 constant_dynamic-update-slice_fusion.5
  50.6 1.0 constant_dynamic-update-slice_fusion.4
  51.6 1.0 constant_dynamic-update-slice_fusion.3
  52.6 1.0 constant_dynamic-update-slice_fusion.2
  53.6 1.0 constant_dynamic-update-slice_fusion.1
  54.6 1.0 constant_dynamic-update-slice_fusion
  55.6 0.0 copy-start.2
  55.6 0.0 copy-start.3
  55.6 22.6 %all-gather.4.cloned.1.call-done = bf16[256,2,3072]{2,0,1:T(8,128)(2,1)} async-done(((bf16[64,2,3072]{2,0,1:T(8,128)(2,1)}), bf16[256,2,3072]{2,0,1:T(8,128)(2,1)}) %all-gather.4.cloned.1.call-update) | async-done | bytes 3145744 | tf_op jit(solution)/shard_map/all_gather | solution.py:20
  78.2 37.7 %all-gather.6.cloned.1.call-done = bf16[3072,1,768]{2,0,1:T(8,128)(2,1)} async-done(((bf16[768,1,768]{2,0,1:T(8,128)(2,1)}), bf16[3072,1,768]{2,0,1:T(8,128)(2,1)}) %all-gather.6.cloned.1.call-update) | async-done | bytes 4718608 | tf_op jit(solution)/shard_map/all_gather | solution.py:24
  115.9 5.9 %fusion = f32[256,2,768]{2,0,1:T(8,128)S(1)} fusion(bf16[256,2,3072]{2,0,1:T(8,128)(2,1)} %all-gather.4.cloned.1.call-done, bf16[3072,1,768]{2,0,1:T(8,128)(2,1)} %all-gather.6.cloned.1.call-done), kind=kOutput, calls=%fused_computation | convolution fusion | flops 2415919104 | bytes 9437184 | tf_op jit(solution)/shard_map/qye,ea->qya/dot_general | solution.py:21
  121.7 0.2 slice_reduce_fusion.1
  122.0 1.7 fusion.15
  123.7 0.4 multiply_reduce_fusion.1
  124.1 0.0 copy-done.2
  124.1 0.0 copy-done.3
  124.1 0.5 fusion.35
  124.6 0.3 fusion.12
  124.9 5.6 %convolution_convert_fusion = bf16[256,2,3072]{2,0,1:T(8,128)(2,1)} fusion(bf16[512,6144]{1,0:T(8,128)(2,1)} %constant_dynamic-update-slice_fusion, s32[]{:T(128)S(6)} %select_n.14, bf16[256,2,384]{2,0,1:T(8,128)(2,1)S(1)} %fusion.15, bf16[256,2,128]{2,0,1:T(8,128)(2,1)S(1)} %fusion.12), kind=kOutput, calls=%fused_computation.2 | convolution fusion | flops 1613234176 | bytes 6815748 | tf_op jit(solution)/shard_map/vto,ox->vtx/dot_general | solution.py:61
  130.5 0.0 copy-start
  130.5 0.0 reduce-scatter.2.cloned.1.call-update
  130.5 60.6 %reduce-scatter.2.cloned.1.call-done = bf16[64,2,3072]{2,0,1:T(8,128)(2,1)} async-done(((bf16[256,2,3072]{2,0,1:T(8,128)(2,1)}), bf16[64,2,3072]{2,0,1:T(8,128)(2,1)}) %reduce-scatter.2.cloned.1.call-update) | async-done | bytes 786448 | tf_op jit(solution)/shard_map/reduce_scatter | solution.py:60
  191.0 0.0 copy-done
  191.0 1.3 fusion.9
  192.4 1.7 copy.8
  (5 shorter events, 0.0 us)
Async XLA Ops:
  6.5 6.1 %copy-start.1 = (bf16[1,512,768]{2,1,0:T(8,128)(2,1)S(1)}, bf16[1,512,768]{2,1,0:T(8,128)(2,1)}, u32[]{:S(2)}) copy-start(bf16[1,512,768]{2,1,0:T(8,128)(2,1)} %param.11) | copy-start | bytes 2359300
  6.5 71.7 %all-gather.4.cloned.1.call-start = ((), (), s32[]{:S(2)}) async-start(), calls=%async_computation.1 | async-start | bytes 3932160 | tf_op jit(solution)/shard_map/all_gather | solution.py:20
  11.9 104.0 %all-gather.6.cloned.1.call-start = ((), (), s32[]{:S(2)}) async-start(), calls=%async_computation.3 | async-start | bytes 5898240 | tf_op jit(solution)/shard_map/all_gather | solution.py:24
  12.6 178.4 %reduce-scatter.2.cloned.1.call-start = ((), (), s32[]{:S(2)}) async-start(), calls=%async_computation.2 | async-start | bytes 3932160 | tf_op jit(solution)/shard_map/reduce_scatter | solution.py:60
  12.7 12.1 %collective-permute-start = (bf16[512,768]{1,0:T(8,128)(2,1)S(1)}, bf16[512,768]{1,0:T(8,128)(2,1)S(1)}, u32[]{:S(2)}, u32[]{:S(2)}) collective-permute-start(bf16[512,768]{1,0:T(8,128)(2,1)S(1)} %bitcast.21), channel_id=1, source_target_pairs={{0,1},{1,2},{2,3},{3,0},{4,5},{5,6},{6,7},{7,4},{8,9},{9,10},{10,1... | collective-permute-start | bytes 2359304 | tf_op jit(solution)/shard_map/ppermute | solution.py:54
  24.8 11.4 %collective-permute-start.1 = (bf16[512,768]{1,0:T(8,128)(2,1)S(1)}, bf16[512,768]{1,0:T(8,128)(2,1)S(1)}, u32[]{:S(2)}, u32[]{:S(2)}) collective-permute-start(bf16[512,768]{1,0:T(8,128)(2,1)S(1)} %collective-permute-done), channel_id=1, source_target_pairs={{0,1},{1,2},{2,3},{3,0},{4,5},{5,6},{6,7},{7,4},{8,9},{9,10},{10,1... | collective-permute-start | bytes 2359304 | tf_op jit(solution)/shard_map/ppermute | solution.py:54
  36.2 11.4 %collective-permute-start.2 = (bf16[512,768]{1,0:T(8,128)(2,1)S(1)}, bf16[512,768]{1,0:T(8,128)(2,1)S(1)}, u32[]{:S(2)}, u32[]{:S(2)}) collective-permute-start(bf16[512,768]{1,0:T(8,128)(2,1)S(1)} %collective-permute-done.1), channel_id=1, source_target_pairs={{0,1},{1,2},{2,3},{3,0},{4,5},{5,6},{6,7},{7,4},{8,9},{9,10},{10,1... | collective-permute-start | bytes 2359304 | tf_op jit(solution)/shard_map/ppermute | solution.py:54
  55.6 68.5 %copy-start.2 = (f32[1,128]{1,0:T(1,128)S(1)}, f32[1,128]{1,0:T(1,128)}, u32[]{:S(2)}) copy-start(f32[1,128]{1,0:T(1,128)} %param.10) | copy-start | bytes 1540
  55.6 68.5 %copy-start.3 = (f32[1,128]{1,0:T(1,128)S(1)}, f32[1,128]{1,0:T(1,128)}, u32[]{:S(2)}) copy-start(f32[1,128]{1,0:T(1,128)} %param.9) | copy-start | bytes 1540
  130.5 60.6 %copy-start = (bf16[64,2,3072]{2,1,0:T(2,128)(2,1)S(1)}, bf16[64,2,3072]{2,1,0:T(2,128)(2,1)}, u32[]{:S(2)}) copy-start(bf16[64,2,3072]{2,1,0:T(2,128)(2,1)} %param.6) | copy-start | bytes 2359300
Sparse Core Ops, SparseCore 0:
  12.0 66.1 all-gather.3
  79.7 36.0 all-gather.5
  130.6 60.3 reduce-scatter.1
